TPU v7x, 8 devices: a whole 2x2x1 slice. The times are simulated.
8 devices in a mesh: batch: 1 (over z), time: 8 (over y, x, core).
Axes of the slice: x: 2, y: 2, z: 1, core: 2. Of those that a mesh axis runs over, the one named last changes fastest.
Arguments:
- latent: bfloat16 [16, 6, 128, 384], P(('batch', 'time'))
- conv_w: bfloat16 [4, 3, 3, 3, 384, 384], replicated
- conv_b: float32 [4, 384], replicated
- norm_g: float32 [5, 384], replicated
- norm_b: float32 [5, 384], replicated
- attn_w: bfloat16 [4, 384, 384], replicated
- attn_b: float32 [4, 384], replicated
Outputs:
- output: bfloat16 [16, 6, 128, 384], P(('batch', 'time'))
All inputs are finite; a program needn't handle non-finite values.
Results may differ from a plain program's by a relative error of at most 0.0124786.
Values are sent between devices in bfloat16 or wider.
A program may use at most 1 GiB of HBM per device.

v0:
```python
import jax
import jax.numpy as jnp
from jax import lax
from jax.sharding import PartitionSpec as P

GROUPS = 32
NORM_EPS = 1e-6


def group_stats(feature):
    channels = feature.shape[-1]
    grouped = feature.reshape(feature.shape[:-1] + (GROUPS, channels // GROUPS)).astype(jnp.float32)
    return jnp.stack([jnp.sum(grouped, axis=(0, 1, 2, 4)), jnp.sum(grouped * grouped, axis=(0, 1, 2, 4))])


def apply_norm(feature, totals, elem_count, norm_gain, norm_shift):
    channels = feature.shape[-1]
    group_mean = totals[0] / elem_count
    inv_std = lax.rsqrt(totals[1] / elem_count - group_mean * group_mean + NORM_EPS)
    mean_full = jnp.repeat(group_mean, channels // GROUPS)
    scale_full = jnp.repeat(inv_std, channels // GROUPS) * norm_gain
    return (feature.astype(jnp.float32) - mean_full) * scale_full + norm_shift


def halo_conv(activation, kernel, conv_bias, group_size):
    prev_frames = lax.ppermute(activation[-2:], "time", [(source, source + 1) for source in range(group_size - 1)])
    first_copy = jnp.broadcast_to(activation[:1], prev_frames.shape)
    prev_frames = jnp.where(lax.axis_index("time") == 0, first_copy, prev_frames)
    padded = jnp.concatenate([prev_frames, activation], axis=0)
    conv_out = lax.conv_general_dilated(padded[None], kernel, (1, 1, 1), ((0, 0), (1, 1), (1, 1)), dimension_numbers=("NDHWC", "DHWIO", "NDHWC"), preferred_element_type=jnp.float32)
    return (conv_out[0] + conv_bias).astype(jnp.bfloat16)


def frame_attention(normed, attn_w, attn_b):
    frames, img_height, img_width, channels = normed.shape
    tokens = normed.reshape(frames, img_height * img_width, channels)
    proj_in = jnp.einsum("fsc,kcd->kfsd", tokens, attn_w[:3], preferred_element_type=jnp.float32)
    proj_in = (proj_in + attn_b[:3, None, None, :]).astype(jnp.bfloat16)
    scores = jnp.einsum("fsd,ftd->fst", proj_in[0], proj_in[1], preferred_element_type=jnp.float32) * channels ** -0.5
    attn_probs = jax.nn.softmax(scores, axis=-1).astype(jnp.bfloat16)
    mixed_val = jnp.einsum("fst,ftd->fsd", attn_probs, proj_in[2], preferred_element_type=jnp.float32).astype(jnp.bfloat16)
    out_proj = jnp.einsum("fsd,de->fse", mixed_val, attn_w[3], preferred_element_type=jnp.float32) + attn_b[3]
    return out_proj.astype(jnp.bfloat16).reshape(normed.shape)


def solution(mesh):
    group_size = mesh.shape["time"]
    video_spec = P(("batch", "time"), None, None, None)

    def device_body(latent, conv_w, conv_b, norm_g, norm_b, attn_w, attn_b):
        frames_dev, img_height, img_width, channels = latent.shape
        elem_count = group_size * frames_dev * img_height * img_width * (channels // GROUPS)

        def norm_full(feature, norm_index):
            totals = lax.psum(group_stats(feature), "time")
            return apply_norm(feature, totals, elem_count, norm_g[norm_index], norm_b[norm_index])

        def resnet_block(feature, norm_first, conv_first):
            activation = jax.nn.silu(norm_full(feature, norm_first)).astype(jnp.bfloat16)
            branch = halo_conv(activation, conv_w[conv_first], conv_b[conv_first], group_size)
            activation = jax.nn.silu(norm_full(branch, norm_first + 1)).astype(jnp.bfloat16)
            branch = halo_conv(activation, conv_w[conv_first + 1], conv_b[conv_first + 1], group_size)
            return feature + branch

        feature = resnet_block(latent, 0, 0)
        normed = norm_full(feature, 2).astype(jnp.bfloat16)
        feature = feature + frame_attention(normed, attn_w, attn_b)
        return resnet_block(feature, 3, 2)

    return jax.shard_map(device_body, mesh=mesh, in_specs=(video_spec, P(), P(), P(), P(), P(), P()), out_specs=video_spec, check_vma=False)
```

profile of v0, /device:TPU:4, one launch (start us, length us, event | category | flops | bytes accessed | tf_op | source)
XLA Modules:
  0.0 349.0 jit_solution(11933465998204261717)
XLA Ops:
  0.0 1.7 convert_reduce_fusion.2
  2.1 24.0 %psum.35 = f32[2,32]{1,0:T(2,128)S(1)} all-reduce(f32[2,32]{1,0:T(2,128)S(1)} %pad_maximum_fusion), channel_id=1, replica_groups=mesh['batch'=1,'time'=8] {'time'}, use_global_device_ids=true, to_apply=%region_4.5 | all-reduce | flops 64 | bytes 512 | tf_op jit(solution)/shard_map/psum | solution.py:55
  26.1 1.5 slice_reduce_fusion.2
  27.6 1.5 slice_reduce_fusion.1
  29.5 2.0 fusion.59
  31.5 2.4 collective-permute-start
  34.1 15.9 %collective-permute-done = bf16[2,6,128,384]{3,2,1,0:T(8,128)(2,1)S(1)} collective-permute-done((bf16[2,6,128,384]{3,2,1,0:T(8,128)(2,1)S(1)}, bf16[2,6,128,384]{3,2,1,0:T(8,128)(2,1)S(1)}, u32[]{:S(2)}, u32[]{:S(2)}) %collective-permute-start) | collective-permute-done | bytes 1179680 | tf_op jit(solution)/shard_map/ppermute | solution.py:26
  50.4 1.8 copy.52
  52.2 0.9 pad.clone
  53.9 22.4 %fusion.45 = (f32[384]{0:T(512)S(1)}, f32[384]{0:T(512)S(1)}, f32[2,6,8,17,384]{4,2,3,1,0:T(8,128)S(1)}) fusion(pred[8,17]{0,1:T(8,128)(4,1)S(1)} %copy-done.7, f32[384]{0:T(512)S(1)} %get-tuple-element.27, bf16[4,3,3,3,384,384]{5,4,3,2,1,0:T(8,128)(2,1)} %param.8, bf16[4,6,1,7,2,384]{5,3,4,1,0,2:T(8,128)(2,1)S(1)} %slice.165, ...), kind=kOutput, calls=%fused_computation.57 | convolution fusion | flops 11565158400 | bytes 13238920 | tf_op jit(solution)/shard_map/conv_general_dilated | solution.py:30
  76.7 22.5 %psum.36 = f32[2,32]{1,0:T(2,128)S(1)} all-reduce(f32[2,32]{1,0:T(2,128)S(1)} %pad_maximum_fusion.1), channel_id=1, replica_groups=mesh['batch'=1,'time'=8] {'time'}, use_global_device_ids=true, to_apply=%region_9.10 | all-reduce | flops 64 | bytes 512 | tf_op jit(solution)/shard_map/psum | solution.py:55
  99.6 1.3 copy.28
  100.9 0.8 slice.166
  101.8 0.8 multiply_convert_fusion.1
  102.5 2.3 collective-permute-start.1
  105.5 15.4 %collective-permute-done.1 = bf16[2,6,128,384]{3,2,1,0:T(8,128)(2,1)S(1)} collective-permute-done((bf16[2,6,128,384]{3,2,1,0:T(8,128)(2,1)S(1)}, bf16[2,6,128,384]{3,2,1,0:T(8,128)(2,1)S(1)}, u32[]{:S(2)}, u32[]{:S(2)}) %collective-permute-start.1) | collective-permute-done | bytes 1179680 | tf_op jit(solution)/shard_map/ppermute | solution.py:26
  121.4 1.8 copy.53
  123.2 0.9 pad.2.clone
  124.6 22.0 %fusion.88 = f32[2,6,8,17,384]{4,2,3,1,0:T(8,128)S(1)} fusion(bf16[4,3,3,3,384,384]{5,4,3,2,1,0:T(8,128)(2,1)} %param.8, bf16[4,6,1,7,2,384]{5,3,4,1,0,2:T(8,128)(2,1)S(1)} %slice.168, bf16[4,6,1,8,17,384]{5,3,4,1,0,2:T(8,128)(2,1)S(1)} %copy.32, pred[8,17]{0,1:T(8,128)(4,1)S(1)} %copy-done.7), kind=kOutput, calls=%fused_computation.109 | convolution fusion | flops 11560144896 | bytes 13234312 | tf_op jit(solution)/shard_map/conv_general_dilated | solution.py:30
  146.6 1.3 copy.33
  147.9 1.2 slice.169
  150.2 23.7 %psum.37 = f32[2,32]{1,0:T(2,128)S(1)} all-reduce(f32[2,32]{1,0:T(2,128)S(1)} %pad_maximum_fusion.2), channel_id=1, replica_groups=mesh['batch'=1,'time'=8] {'time'}, use_global_device_ids=true, to_apply=%region_14.15 | all-reduce | flops 64 | bytes 512 | tf_op jit(solution)/shard_map/psum | solution.py:55
  174.7 3.3 fusion.18
  178.0 1.7 copy-done.2
  179.7 1.4 fusion.110
  181.2 2.1 copy-done.1
  183.3 1.3 fusion.150
  184.5 6.9 %add_convert_fusion.3 = bf16[2,768,384]{2,1,0:T(8,128)(2,1)S(1)} fusion(f32[2,768]{1,0:T(2,128)S(1)} %fusion.150, bf16[3,2,768,384]{3,2,0,1:T(8,128)(2,1)} %copy-done.2, f32[384]{0:T(512)S(1)} %copy-done.5, bf16[4,384,384]{2,1,0:T(8,128)(2,1)} %param.12, f32[2,768,768]{1,2,0:T(8,128)} %copy-done.1), kind=kOutput, calls=%fused_computation.104 | convolution fusion | flops 1366624512 | bytes 12099072 | tf_op jit(solution)/shard_map/fsd,de->fse/dot_general | solution.py:42
  191.4 1.2 convert_reduce_fusion
  192.6 0.8 reduce_sum.189
  193.7 23.4 %psum.38 = f32[2,32]{1,0:T(2,128)S(1)} all-reduce(f32[2,32]{1,0:T(2,128)S(1)} %pad_maximum_fusion.3), channel_id=1, replica_groups=mesh['batch'=1,'time'=8] {'time'}, use_global_device_ids=true, to_apply=%region_21.22 | all-reduce | flops 64 | bytes 512 | tf_op jit(solution)/shard_map/psum | solution.py:55
  218.1 1.4 fusion.72
  219.6 2.1 collective-permute-start.2
  221.8 16.2 %collective-permute-done.2 = bf16[2,6,128,384]{3,2,1,0:T(8,128)(2,1)S(1)} collective-permute-done((bf16[2,6,128,384]{3,2,1,0:T(8,128)(2,1)S(1)}, bf16[2,6,128,384]{3,2,1,0:T(8,128)(2,1)S(1)}, u32[]{:S(2)}, u32[]{:S(2)}) %collective-permute-start.2) | collective-permute-done | bytes 1179680 | tf_op jit(solution)/shard_map/ppermute | solution.py:26
  238.4 1.8 copy.54
  240.3 0.9 pad.4.clone
  241.9 30.6 %fusion.48 = (f32[384]{0:T(512)S(1)}, f32[384]{0:T(512)S(1)}, f32[2,6,8,17,384]{4,2,3,1,0:T(8,128)}) fusion(pred[8,17]{0,1:T(8,128)(4,1)S(1)} %copy-done.8, f32[384]{0:T(512)S(1)} %get-tuple-element.28, bf16[4,3,3,3,384,384]{5,4,3,2,1,0:T(8,128)(2,1)} %param.8, bf16[4,6,1,7,2,384]{5,3,4,1,0,2:T(8,128)(2,1)S(1)} %slice.174, ...), kind=kOutput, calls=%fused_computation.60 | convolution fusion | flops 11565158400 | bytes 13238920 | tf_op jit(solution)/shard_map/conv_general_dilated | solution.py:30
  272.9 23.2 %psum.39 = f32[2,32]{1,0:T(2,128)S(1)} all-reduce(f32[2,32]{1,0:T(2,128)S(1)} %pad_maximum_fusion.4), channel_id=1, replica_groups=mesh['batch'=1,'time'=8] {'time'}, use_global_device_ids=true, to_apply=%region_26.27 | all-reduce | flops 64 | bytes 512 | tf_op jit(solution)/shard_map/psum | solution.py:55
  296.6 3.0 copy.39
  299.6 0.8 slice.175
  301.2 1.9 collective-permute-start.3
  303.2 16.4 %collective-permute-done.3 = bf16[2,6,128,384]{3,2,1,0:T(8,128)(2,1)S(1)} collective-permute-done((bf16[2,6,128,384]{3,2,1,0:T(8,128)(2,1)S(1)}, bf16[2,6,128,384]{3,2,1,0:T(8,128)(2,1)S(1)}, u32[]{:S(2)}, u32[]{:S(2)}) %collective-permute-start.3) | collective-permute-done | bytes 1179680 | tf_op jit(solution)/shard_map/ppermute | solution.py:26
  320.0 1.8 copy.55
  321.8 0.9 pad.6.clone
  323.2 22.1 %fusion.98 = f32[2,6,8,17,384]{4,2,3,1,0:T(8,128)S(1)} fusion(bf16[4,3,3,3,384,384]{5,4,3,2,1,0:T(8,128)(2,1)} %param.8, bf16[4,6,1,7,2,384]{5,3,4,1,0,2:T(8,128)(2,1)S(1)} %slice.177, bf16[4,6,1,8,17,384]{5,3,4,1,0,2:T(8,128)(2,1)S(1)} %copy.43, pred[8,17]{0,1:T(8,128)(4,1)S(1)} %copy-done.8), kind=kOutput, calls=%fused_computation.111 | convolution fusion | flops 11560144896 | bytes 13234312 | tf_op jit(solution)/shard_map/conv_general_dilated | solution.py:30
  345.3 1.3 copy.44
  346.6 0.8 slice.178
  347.4 1.4 fusion.109
  (100 shorter events, 11.1 us)
Async XLA Ops:
  0.0 33.9 %copy-start.4 = (f32[4,384]{1,0:T(4,128)S(1)}, f32[4,384]{1,0:T(4,128)}, u32[]{:S(2)}) copy-start(f32[4,384]{1,0:T(4,128)} %param.9) | copy-start | bytes 18436
  31.5 18.4 %collective-permute-start = (bf16[2,6,128,384]{3,2,1,0:T(8,128)(2,1)S(1)}, bf16[2,6,128,384]{3,2,1,0:T(8,128)(2,1)S(1)}, u32[]{:S(2)}, u32[]{:S(2)}) collective-permute-start(bf16[2,6,128,384]{3,2,1,0:T(8,128)(2,1)S(1)} %fusion.59), channel_id=1, source_target_pairs={{0,1},{1,2},{2,3},{3,4},{4,5},{5,6},{6,7}} | collective-permute-start | bytes 3538952 | tf_op jit(solution)/shard_map/ppermute | solution.py:26
  53.2 0.7 copy-start.7
  101.8 3.1 copy-start.6
  102.5 18.4 %collective-permute-start.1 = (bf16[2,6,128,384]{3,2,1,0:T(8,128)(2,1)S(1)}, bf16[2,6,128,384]{3,2,1,0:T(8,128)(2,1)S(1)}, u32[]{:S(2)}, u32[]{:S(2)}) collective-permute-start(bf16[2,6,128,384]{3,2,1,0:T(8,128)(2,1)S(1)} %multiply_convert_fusion.1), channel_id=1, source_target_pairs={{0,1},{1,2},{2,3},{3,4},{4,5},{5,6},{6,7}} | collective-permute-start | bytes 3538952 | tf_op jit(solution)/shard_map/ppermute | solution.py:26
  147.9 1.3 copy-start
  178.0 1.8 copy-start.2
  181.1 2.1 copy-start.1
  183.3 1.3 copy-start.5
  219.6 18.4 %collective-permute-start.2 = (bf16[2,6,128,384]{3,2,1,0:T(8,128)(2,1)S(1)}, bf16[2,6,128,384]{3,2,1,0:T(8,128)(2,1)S(1)}, u32[]{:S(2)}, u32[]{:S(2)}) collective-permute-start(bf16[2,6,128,384]{3,2,1,0:T(8,128)(2,1)S(1)} %fusion.72), channel_id=1, source_target_pairs={{0,1},{1,2},{2,3},{3,4},{4,5},{5,6},{6,7}} | collective-permute-start | bytes 3538952 | tf_op jit(solution)/shard_map/ppermute | solution.py:26
  241.2 0.7 copy-start.8
  299.6 0.8 copy-start.3
  301.2 18.4 %collective-permute-start.3 = (bf16[2,6,128,384]{3,2,1,0:T(8,128)(2,1)S(1)}, bf16[2,6,128,384]{3,2,1,0:T(8,128)(2,1)S(1)}, u32[]{:S(2)}, u32[]{:S(2)}) collective-permute-start(bf16[2,6,128,384]{3,2,1,0:T(8,128)(2,1)S(1)} %multiply_convert_fusion), channel_id=1, source_target_pairs={{0,1},{1,2},{2,3},{3,4},{4,5},{5,6},{6,7}} | collective-permute-start | bytes 3538952 | tf_op jit(solution)/shard_map/ppermute | solution.py:26
where the time goes:
time: 353 us; the launch traced here: 349 us
  blocking collectives  117 us (33%)
  matrix products  109 us (31%)
  waiting for transfers between devices  64 us (18%)
  local copies, waits for them, and re-layouts  35 us (10%)
  other arithmetic  15 us (4%)
  starting transfers between devices  8.73 us (2%)
    psum x5, blocking collectives, norm_full(): totals = lax.psum(group_stats(feature), 'time')  117 us
    conv_general_dilated x4, matrix products, halo_conv(): lax.conv_general_dilated(padded[None], kernel, (1, 1, 1), ((0, 0), (1, 1)...  97.1 us
    ppermute x4, waiting for transfers between devices, halo_conv(): lax.ppermute(activation[-2:], 'time', [(source, source + 1) for source in...  64 us
    conv_general_dilated x16, local copies, waits for them, and re-layouts, halo_conv(): lax.conv_general_dilated(padded[None], kernel, (1, 1, 1), ((0, 0), (1, 1)...  12.1 us
    unnamed x22, local copies, waits for them, and re-layouts  11.8 us
    ppermute x4, starting transfers between devices, halo_conv(): lax.ppermute(activation[-2:], 'time', [(source, source + 1) for source in...  8.73 us
  transfers between devices with their start and end apart: 4, of which 4 were waited for; matrix products, arithmetic and copies ran while one was open for 0% of the time, Pallas kernels for 0%

commit v1 on v0

v1 whole, which is shorter than its diff:
```python
import functools

import jax
import jax.numpy as jnp
from jax import lax
from jax.experimental import pallas as pl
from jax.experimental.pallas import tpu as pltpu
from jax.sharding import PartitionSpec as P

GROUPS = 32
NORM_EPS = 1e-6
MESH = pl.DeviceIdType.MESH


def dot(a, b):
    return jnp.dot(a, b, preferred_element_type=jnp.float32)


def block_kernel(
    n, height, width, chans,
    latent, conv_w, conv_b, norm_g, norm_b, attn_w, attn_b, out,
    wbuf, awbuf, cbuf, gbuf, bbuf, abuf, umap, src, xres, land, acc, qkv, stat_out, stat_in,
    w_sem, p_sem, x_sem, o_sem, halo_send, halo_recv, st_send, st_recv,
):
    pos = height * width
    taps = 27
    lanes = chans // 128
    group = chans // GROUPS
    elems = n * 2 * pos * group
    me = lax.axis_index("time")
    inner = lax.min(me, 1)
    slot_m1, slot_m2 = 2 - inner, 2 - 2 * inner

    def x_copy(f):
        return pltpu.make_async_copy(latent.at[f], src.at[f], x_sem.at[f])

    def w_copy(k):
        return pltpu.make_async_copy(conv_w.at[k], wbuf.at[k], w_sem.at[k])

    small = [
        pltpu.make_async_copy(a, b, p_sem.at[i])
        for i, (a, b) in enumerate([(norm_g, gbuf), (norm_b, bbuf), (conv_b, cbuf), (attn_b, abuf)])
    ]
    aw_copy = pltpu.make_async_copy(attn_w, awbuf, p_sem.at[4])
    for f in range(2):
        x_copy(f).start()
    for c in small:
        c.start()
    for k in range(4):
        w_copy(k).start()
    aw_copy.start()

    barrier = pltpu.get_barrier_semaphore()
    for d in range(1, n):
        pl.semaphore_signal(barrier, inc=1, device_id={"time": lax.rem(me + d, n)}, device_id_type=MESH)

    zero_row = jnp.zeros((width, chans), jnp.bfloat16)
    for s in range(4):
        umap[s, 0:width, :] = zero_row
        umap[s, width + pos : 2 * width + pos, :] = zero_row

    def put_stats(index, s1, s2):
        rows = [jnp.sum(s[:, 128 * b : 128 * b + 128], axis=0, keepdims=True) for s in (s1, s2) for b in range(lanes)]
        rows.append(jnp.zeros((8 - 2 * lanes, 128), jnp.float32))
        stat_out[index] = jnp.concatenate(rows, axis=0)

    def add_stats(carry, v):
        s1, s2 = carry
        t = v.reshape(v.shape[0] // 8, 8, v.shape[1])
        return s1 + jnp.sum(t, axis=0), s2 + jnp.sum(t * t, axis=0)

    zero_stats = (jnp.zeros((8, chans), jnp.float32),) * 2

    def stat_copy(index, d):
        return pltpu.make_async_remote_copy(
            src_ref=stat_out.at[index],
            dst_ref=stat_in.at[index, me],
            send_sem=st_send.at[index, d],
            recv_sem=st_recv.at[index, d],
            device_id={"time": lax.rem(me + d, n)},
            device_id_type=MESH,
        )

    def norm_params(index):
        for d in range(1, n):
            stat_copy(index, d).start()
        stat_in[index, me] = stat_out[index]
        for d in range(1, n):
            stat_copy(index, d).wait()
        total = stat_in[index, 0]
        for d in range(1, n):
            total = total + stat_in[index, d]
        lane = lax.broadcasted_iota(jnp.int32, (8, 128), 1)
        chan = lane + 128 * lax.rem(lax.broadcasted_iota(jnp.int32, (8, 128), 0), lanes)
        place = lax.rem(chan, group)
        sums = jnp.zeros((8, 128), jnp.float32)
        for s in range(1 - group, group):
            moved = pltpu.roll(total, (-s) % 128, 1) if s else total
            if s > 0:
                moved = jnp.where(lane >= 128 - s, pltpu.roll(moved, 7, 0), moved)
            elif s < 0:
                moved = jnp.where(lane < -s, pltpu.roll(moved, 1, 0), moved)
            sums = sums + jnp.where((place + s >= 0) & (place + s < group), moved, 0.0)
        mean = jnp.concatenate([sums[b : b + 1] for b in range(lanes)], axis=1) / elems
        square = jnp.concatenate([sums[lanes + b : lanes + b + 1] for b in range(lanes)], axis=1) / elems
        scale = lax.rsqrt(square - mean * mean + NORM_EPS) * gbuf[pl.ds(index, 1), :]
        return mean, scale, bbuf[pl.ds(index, 1), :]

    def normed(v, params):
        mean, scale, shift = params
        return (v.astype(jnp.float32) - mean) * scale + shift

    def activate(v, params):
        y = 0.5 * normed(v, params)
        return (y + y * jnp.tanh(y)).astype(jnp.bfloat16)

    def fill(slot, read, params):
        def row(i, _):
            at = pl.multiple_of(i * width, width)
            umap[slot, pl.ds(at + width, width), :] = activate(read(at), params)
            return 0

        lax.fori_loop(0, height, row, 0)

    def halo_copy(k, f):
        return pltpu.make_async_remote_copy(
            src_ref=src.at[f],
            dst_ref=land.at[k, f],
            send_sem=halo_send.at[k, f],
            recv_sem=halo_recv.at[k, f],
            device_id={"time": lax.min(me + 1, n - 1)},
            device_id_type=MESH,
        )

    def send_halo(k, f):
        @pl.when(me < n - 1)
        def _():
            halo_copy(k, f).start()

    def lhs(slot):
        return jnp.concatenate([umap[slot, d * width : d * width + pos, :] for d in range(3)], axis=1)

    def rhs(k, a, e):
        return jnp.concatenate([wbuf[k, a * 9 + d * 3 + e] for d in range(3)], axis=0)

    def both_outs(k, slot, a0, first):
        def step(e, _):
            part = dot(lhs(slot), jnp.concatenate([rhs(k, a0, e), rhs(k, a0 - 1, e)], axis=1))
            acc[e] = part if first else acc[e] + part
            return 0

        lax.fori_loop(0, 3, step, 0)

    def one_out(k, slot, a, o):
        part = dot(lhs(slot), jnp.concatenate([rhs(k, a, e) for e in range(3)], axis=1))
        for e in range(3):
            acc[e, :, o * chans : (o + 1) * chans] += part[:, e * chans : (e + 1) * chans]

    def finish(k, o, stats):
        column = lax.broadcasted_iota(jnp.int32, (width, 1), 0)
        bias = cbuf[pl.ds(k, 1), :]
        odd = lax.rem(k, 2) == 1

        def row(i, carry):
            at = pl.ds(pl.multiple_of(i * width, width), width)
            cols = slice(o * chans, (o + 1) * chans)
            left = jnp.where(column == 0, 0.0, pltpu.roll(acc[0, at, cols], 1, 0))
            right = jnp.where(column == width - 1, 0.0, pltpu.roll(acc[2, at, cols], width - 1, 0))
            h = (acc[1, at, cols] + left + right + bias).astype(jnp.bfloat16).astype(jnp.float32)
            old = xres[o, at, :]
            new = jnp.where(odd, h + old.astype(jnp.float32), h).astype(jnp.bfloat16)
            src[o, at, :] = new
            xres[o, at, :] = jnp.where(odd, new, old)
            return add_stats(carry, new.astype(jnp.float32))

        return lax.fori_loop(0, height, row, stats)

    def out_copy(f):
        return pltpu.make_async_copy(src.at[f], out.at[f], o_sem.at[f])

    def attention():
        params = norm_params(2)
        aw_copy.wait()
        part_rows = pos // 3

        def frame(t, carry):
            f = 1 - t

            def project(i, _):
                at = pl.ds(pl.multiple_of(i * part_rows, part_rows), part_rows)
                a = normed(xres[f, at, :], params).astype(jnp.bfloat16)
                w = jnp.concatenate([awbuf[0], awbuf[1], awbuf[2]], axis=1)
                b = jnp.concatenate([abuf[j : j + 1] for j in range(3)], axis=1)
                qkv[at, :] = (dot(a, w) + b).astype(jnp.bfloat16)
                return 0

            lax.fori_loop(0, 3, project, 0)

            def attend(i, carry):
                at = pl.ds(pl.multiple_of(i * part_rows, part_rows), part_rows)
                scores = lax.dot_general(
                    qkv[at, 0:chans], qkv[:, chans : 2 * chans], (((1,), (1,)), ((), ())), preferred_element_type=jnp.float32
                ) * chans ** -0.5
                top = jnp.max(scores, axis=1, keepdims=True)
                e = jnp.exp(scores - top)
                p = (e / jnp.sum(e, axis=1, keepdims=True)).astype(jnp.bfloat16)
                o = dot(p, qkv[:, 2 * chans : 3 * chans]).astype(jnp.bfloat16)
                h = (dot(o, awbuf[3]) + abuf[3:4]).astype(jnp.bfloat16)
                new = (xres[f, at, :].astype(jnp.float32) + h.astype(jnp.float32)).astype(jnp.bfloat16)
                src[f, at, :] = new
                xres[f, at, :] = new
                return add_stats(carry, new.astype(jnp.float32))

            carry = lax.fori_loop(0, 3, attend, carry)
            send_halo(2, f)
            return carry

        put_stats(3, *lax.fori_loop(0, 2, frame, zero_stats))

    for f in range(2):
        x_copy(f).wait()

    def first_row(i, carry):
        for f in range(2):
            at = pl.ds(pl.multiple_of(i * width, width), width)
            v = src[f, at, :]
            xres[f, at, :] = v
            carry = add_stats(carry, v.astype(jnp.float32))
        return carry

    put_stats(0, *lax.fori_loop(0, height, first_row, zero_stats))
    for c in small:
        c.wait()
    pl.semaphore_wait(barrier, n - 1)
    for f in (1, 0):
        send_halo(0, f)

    def stage(k, _):
        index = k + lax.div(k, 2)
        params = norm_params(index)
        for f in range(2):
            fill(2 + f, lambda at: src[f, pl.ds(at, width), :], params)
        w_copy(k).wait()
        both_outs(k, 2, 2, True)
        one_out(k, 3, 2, 1)

        @pl.when(me > 0)
        def _():
            halo_copy(k, 1).wait_recv()
            fill(1, lambda at: land[k, 1, pl.ds(at, width), :], params)

        both_outs(k, slot_m1, 1, False)

        @pl.when(me < n - 1)
        def _():
            halo_copy(k, 1).wait_send()

        stats = finish(k, 1, zero_stats)

        @pl.when(lax.rem(k, 2) == 0)
        def _():
            send_halo(k + 1, 1)

        @pl.when(k == 3)
        def _():
            out_copy(1).start()

        @pl.when(me > 0)
        def _():
            halo_copy(k, 0).wait_recv()
            fill(0, lambda at: land[k, 0, pl.ds(at, width), :], params)

        one_out(k, slot_m2, 0, 0)

        @pl.when(me < n - 1)
        def _():
            halo_copy(k, 0).wait_send()

        stats = finish(k, 0, stats)

        @pl.when(lax.rem(k, 2) == 0)
        def _():
            send_halo(k + 1, 0)

        @pl.when(k == 3)
        def _():
            out_copy(0).start()

        put_stats(lax.min(index + 1, 4), *stats)

        @pl.when(k == 1)
        def _():
            attention()

        return 0

    lax.fori_loop(0, 4, stage, 0)
    for f in range(2):
        out_copy(f).wait()


def solution(mesh):
    n = mesh.shape["time"]
    video_spec = P(("batch", "time"), None, None, None)

    def device_body(latent, conv_w, conv_b, norm_g, norm_b, attn_w, attn_b):
        frames, height, width, chans = latent.shape
        pos = height * width
        bf16, f32 = jnp.bfloat16, jnp.float32
        out = pl.pallas_call(
            functools.partial(block_kernel, n, height, width, chans),
            out_shape=jax.ShapeDtypeStruct((frames, pos, chans), bf16),
            in_specs=[pl.BlockSpec(memory_space=pl.ANY)] * 7,
            out_specs=pl.BlockSpec(memory_space=pl.ANY),
            scratch_shapes=[
                pltpu.VMEM((4, 27, chans, chans), bf16),
                pltpu.VMEM((4, chans, chans), bf16),
                pltpu.VMEM((4, chans), f32),
                pltpu.VMEM((5, chans), f32),
                pltpu.VMEM((5, chans), f32),
                pltpu.VMEM((4, chans), f32),
                pltpu.VMEM((4, pos + 2 * width, chans), bf16),
                pltpu.VMEM((2, pos, chans), bf16),
                pltpu.VMEM((2, pos, chans), bf16),
                pltpu.VMEM((4, 2, pos, chans), bf16),
                pltpu.VMEM((3, pos, 2 * chans), f32),
                pltpu.VMEM((pos, 3 * chans), bf16),
                pltpu.VMEM((5, 8, 128), f32),
                pltpu.VMEM((5, n, 8, 128), f32),
                pltpu.SemaphoreType.DMA((4,)),
                pltpu.SemaphoreType.DMA((5,)),
                pltpu.SemaphoreType.DMA((2,)),
                pltpu.SemaphoreType.DMA((2,)),
                pltpu.SemaphoreType.DMA((4, 2)),
                pltpu.SemaphoreType.DMA((4, 2)),
                pltpu.SemaphoreType.DMA((5, n)),
                pltpu.SemaphoreType.DMA((5, n)),
            ],
            compiler_params=pltpu.CompilerParams(collective_id=0, has_side_effects=True, vmem_limit_bytes=67043328),
            name="mid_block",
        )(latent.reshape(frames, pos, chans), conv_w.reshape(4, 27, chans, chans), conv_b, norm_g, norm_b, attn_w, attn_b)
        return out.reshape(latent.shape)

    return jax.shard_map(device_body, mesh=mesh, in_specs=(video_spec, P(), P(), P(), P(), P(), P()), out_specs=video_spec, check_vma=False)
```

time: 353 us -> 152 us (0.43)
  the two profiles are of different devices: /device:TPU:4 before, /device:TPU:0 now
where the time goes in v1:
time: 152 us; the launch traced here: 151 us
  Pallas kernels  149 us (98%)
  local copies, waits for them, and re-layouts  2.41 us (2%)
    pallas_call x1, Pallas kernels, device_body(): pl.pallas_call(functools.partial(block_kernel, n, height, width, chans),...  149 us

profile of v1, /device:TPU:0, one launch (start us, length us, event | category | flops | bytes accessed | tf_op | source)
XLA Modules:
  0.0 151.4 jit_solution(7894918042012003764)
XLA Ops:
  0.0 149.0 %mid_block.1 = bf16[2,768,384]{2,1,0:T(8,128)(2,1)} custom-call(bf16[2,768,384]{2,1,0:T(8,128)(2,1)} %bitcast.5, bf16[4,27,384,384]{3,2,1,0:T(8,128)(2,1)} %bitcast.3, f32[4,384]{1,0:T(4,128)} %conv_b.1, f32[5,384]{1,0:T(8,128)} %norm_g.1, f32[5,384]{1,0:T(8,128)} %norm_b.1, bf16[4,384,384]{2,1,0:T(8,128)(2,1)} %attn_w.1, f32[4,384]{1,0:T(4,128)} %attn_b.1), custom_call_target="tpu_custom_call" | custom-call | tf_op jit(solution)/shard_map/mid_block/pallas_call | solution.py:310
  149.0 2.4 %copy.9 = bf16[2,6,128,384]{3,2,1,0:T(8,128)(2,1)} copy(bf16[2,6,128,384]{3,2,1,0:T(8,128)(2,1)} %bitcast.4) | data formatting | bytes 2359296

commit v2 on v1

--- a/solution.py
+++ b/solution.py
@@ -16,11 +16,17 @@
     return jnp.dot(a, b, preferred_element_type=jnp.float32)
 
 
+def copy_kernel(a, out, sem):
+    c = pltpu.make_async_copy(a, out, sem)
+    c.start()
+    c.wait()
+
+
 def block_kernel(
     n, height, width, chans,
     latent, conv_w, conv_b, norm_g, norm_b, attn_w, attn_b, out,
-    wbuf, awbuf, cbuf, gbuf, bbuf, abuf, umap, src, xres, land, acc, qkv, stat_out, stat_in,
-    w_sem, p_sem, x_sem, o_sem, halo_send, halo_recv, st_send, st_recv,
+    wbuf, awbuf, cbuf, gbuf, bbuf, abuf, u_m2, u_m1, u_0, u_1, src, xres, land, acc, qkv, stat_out, stat_in,
+    w_sem, p_sem, x_sem, halo_send, halo_recv, st_send, st_recv,
 ):
     pos = height * width
     taps = 27
@@ -28,8 +34,7 @@
     group = chans // GROUPS
     elems = n * 2 * pos * group
     me = lax.axis_index("time")
-    inner = lax.min(me, 1)
-    slot_m1, slot_m2 = 2 - inner, 2 - 2 * inner
+    umaps = (u_m2, u_m1, u_0, u_1)
 
     def x_copy(f):
         return pltpu.make_async_copy(latent.at[f], src.at[f], x_sem.at[f])
@@ -55,9 +60,9 @@
         pl.semaphore_signal(barrier, inc=1, device_id={"time": lax.rem(me + d, n)}, device_id_type=MESH)
 
     zero_row = jnp.zeros((width, chans), jnp.bfloat16)
-    for s in range(4):
-        umap[s, 0:width, :] = zero_row
-        umap[s, width + pos : 2 * width + pos, :] = zero_row
+    for u in umaps:
+        u[0:width, :] = zero_row
+        u[width + pos : 2 * width + pos, :] = zero_row
 
     def put_stats(index, s1, s2):
         rows = [jnp.sum(s[:, 128 * b : 128 * b + 128], axis=0, keepdims=True) for s in (s1, s2) for b in range(lanes)]
@@ -81,9 +86,11 @@
             device_id_type=MESH,
         )
 
-    def norm_params(index):
+    def norm_params(index, sent=None):
         for d in range(1, n):
             stat_copy(index, d).start()
+        if sent is not None:
+            sent()
         stat_in[index, me] = stat_out[index]
         for d in range(1, n):
             stat_copy(index, d).wait()
@@ -114,69 +121,96 @@
         y = 0.5 * normed(v, params)
         return (y + y * jnp.tanh(y)).astype(jnp.bfloat16)
 
-    def fill(slot, read, params):
-        def row(i, _):
-            at = pl.multiple_of(i * width, width)
-            umap[slot, pl.ds(at + width, width), :] = activate(read(at), params)
-            return 0
-
-        lax.fori_loop(0, height, row, 0)
-
-    def halo_copy(k, f):
+    def fill(u, read, params):
+        for i in range(height):
+            u[(i + 1) * width : (i + 2) * width, :] = activate(read(i * width), params)
+
+    def own(f):
+        return lambda at: src[f, at : at + width, :]
+
+    def halo(k, f):
+        return lambda at: jnp.where(me == 0, src[0, at : at + width, :], land[k, f, at : at + width, :])
+
+    half = pos // 2
+    parts = ((1, 0, half), (1, half, half), (0, 0, pos))
+
+    def halo_copy(k, part):
+        f, at, rows = parts[part]
         return pltpu.make_async_remote_copy(
-            src_ref=src.at[f],
-            dst_ref=land.at[k, f],
-            send_sem=halo_send.at[k, f],
-            recv_sem=halo_recv.at[k, f],
+            src_ref=src.at[f, pl.ds(at, rows)],
+            dst_ref=land.at[k, f, pl.ds(at, rows)],
+            send_sem=halo_send.at[k, part],
+            recv_sem=halo_recv.at[k, part],
             device_id={"time": lax.min(me + 1, n - 1)},
             device_id_type=MESH,
         )
 
-    def send_halo(k, f):
+    def send_halo(k, *which):
         @pl.when(me < n - 1)
         def _():
-            halo_copy(k, f).start()
-
-    def lhs(slot):
-        return jnp.concatenate([umap[slot, d * width : d * width + pos, :] for d in range(3)], axis=1)
-
-    def rhs(k, a, e):
-        return jnp.concatenate([wbuf[k, a * 9 + d * 3 + e] for d in range(3)], axis=0)
-
-    def both_outs(k, slot, a0, first):
-        def step(e, _):
-            part = dot(lhs(slot), jnp.concatenate([rhs(k, a0, e), rhs(k, a0 - 1, e)], axis=1))
-            acc[e] = part if first else acc[e] + part
-            return 0
-
-        lax.fori_loop(0, 3, step, 0)
-
-    def one_out(k, slot, a, o):
-        part = dot(lhs(slot), jnp.concatenate([rhs(k, a, e) for e in range(3)], axis=1))
-        for e in range(3):
-            acc[e, :, o * chans : (o + 1) * chans] += part[:, e * chans : (e + 1) * chans]
+            for part in which:
+                halo_copy(k, part).start()
+
+    def halo_sent(k, *which):
+        @pl.when(me < n - 1)
+        def _():
+            for part in which:
+                halo_copy(k, part).wait_send()
+
+    def halo_here(k, *which):
+        @pl.when(me > 0)
+        def _():
+            for part in which:
+                halo_copy(k, part).wait_recv()
+
+    column = lax.broadcasted_iota(jnp.int32, (width, 1), 0)
+
+    spans = ((1, height - 1, (0, 1, 2)), (0, 1, (1, 2)), (height - 1, height, (0, 1)))
+
+    def lhs(span, *us):
+        top, end, ds = span
+        return jnp.concatenate([u[(d + top) * width : (d + end) * width, :] for u in us for d in ds], axis=1)
+
+    def rhs(span, k, a, e):
+        return jnp.concatenate([wbuf[k, a * 9 + d * 3 + e] for d in span[2]], axis=0)
+
+    def add_shifted(span, part, e, cols, first=False):
+        for i in range(span[0], span[1]):
+            at = slice(i * width, (i + 1) * width)
+            v = part[(i - span[0]) * width : (i - span[0] + 1) * width]
+            if e == 0:
+                v = jnp.where(column == 0, 0.0, pltpu.roll(v, 1, 0))
+            elif e == 2:
+                v = jnp.where(column == width - 1, 0.0, pltpu.roll(v, width - 1, 0))
+            acc[at, cols] = v if first else acc[at, cols] + v
+
+    outs = [slice(o * chans, (o + 1) * chans) for o in range(2)]
+
+    def one_out(k, u, a, o, first):
+        for span in spans:
+            part = dot(lhs(span, u), jnp.concatenate([rhs(span, k, a, e) for e in range(3)], axis=1))
+            for e in range(3):
+                add_shifted(span, part[:, e * chans : (e + 1) * chans], e, outs[o], first and e == 0)
+
+    def both_outs(k, e, *frames, first=False):
+        for span in spans:
+            w = [jnp.concatenate([rhs(span, k, 2 - f, e), rhs(span, k, 1 - f, e)], axis=1) for f in frames]
+            part = dot(lhs(span, *((u_0, u_m1)[f] for f in frames)), jnp.concatenate(w, axis=0))
+            for o in range(2):
+                add_shifted(span, part[:, outs[o]], e, outs[o], o == 0 and first)
 
     def finish(k, o, stats):
-        column = lax.broadcasted_iota(jnp.int32, (width, 1), 0)
         bias = cbuf[pl.ds(k, 1), :]
         odd = lax.rem(k, 2) == 1
-
-        def row(i, carry):
-            at = pl.ds(pl.multiple_of(i * width, width), width)
-            cols = slice(o * chans, (o + 1) * chans)
-            left = jnp.where(column == 0, 0.0, pltpu.roll(acc[0, at, cols], 1, 0))
-            right = jnp.where(column == width - 1, 0.0, pltpu.roll(acc[2, at, cols], width - 1, 0))
-            h = (acc[1, at, cols] + left + right + bias).astype(jnp.bfloat16).astype(jnp.float32)
+        for i in range(height):
+            at = slice(i * width, (i + 1) * width)
+            h = (acc[at, outs[o]] + bias).astype(jnp.bfloat16).astype(jnp.float32)
             old = xres[o, at, :]
             new = jnp.where(odd, h + old.astype(jnp.float32), h).astype(jnp.bfloat16)
             src[o, at, :] = new
             xres[o, at, :] = jnp.where(odd, new, old)
-            return add_stats(carry, new.astype(jnp.float32))
-
-        return lax.fori_loop(0, height, row, stats)
-
-    def out_copy(f):
-        return pltpu.make_async_copy(src.at[f], out.at[f], o_sem.at[f])
+            stats = add_stats(stats, new.astype(jnp.float32))
+        return stats
 
     def attention():
         params = norm_params(2)
@@ -212,7 +246,11 @@
                 return add_stats(carry, new.astype(jnp.float32))
 
             carry = lax.fori_loop(0, 3, attend, carry)
-            send_halo(2, f)
+
+            @pl.when(t == 0)
+            def _():
+                send_halo(2, 0)
+
             return carry
 
         put_stats(3, *lax.fori_loop(0, 2, frame, zero_stats))
@@ -232,60 +270,33 @@
     for c in small:
         c.wait()
     pl.semaphore_wait(barrier, n - 1)
-    for f in (1, 0):
-        send_halo(0, f)
+    send_halo(0, 0)
 
     def stage(k, _):
         index = k + lax.div(k, 2)
-        params = norm_params(index)
-        for f in range(2):
-            fill(2 + f, lambda at: src[f, pl.ds(at, width), :], params)
+        params = norm_params(index, lambda: send_halo(k, 1, 2))
+        fill(u_1, own(1), params)
         w_copy(k).wait()
-        both_outs(k, 2, 2, True)
-        one_out(k, 3, 2, 1)
-
-        @pl.when(me > 0)
-        def _():
-            halo_copy(k, 1).wait_recv()
-            fill(1, lambda at: land[k, 1, pl.ds(at, width), :], params)
-
-        both_outs(k, slot_m1, 1, False)
-
-        @pl.when(me < n - 1)
-        def _():
-            halo_copy(k, 1).wait_send()
-
+        fill(u_0, own(0), params)
+        one_out(k, u_1, 2, 1, True)
+        halo_here(k, 0, 1)
+        both_outs(k, 0, 0, first=True)
+        fill(u_m1, halo(k, 1), params)
+        both_outs(k, 0, 1)
+        both_outs(k, 1, 0, 1)
+        halo_here(k, 2)
+        fill(u_m2, halo(k, 0), params)
+        both_outs(k, 2, 0, 1)
+        halo_sent(k, 0, 1)
         stats = finish(k, 1, zero_stats)
 
         @pl.when(lax.rem(k, 2) == 0)
         def _():
-            send_halo(k + 1, 1)
-
-        @pl.when(k == 3)
-        def _():
-            out_copy(1).start()
-
-        @pl.when(me > 0)
-        def _():
-            halo_copy(k, 0).wait_recv()
-            fill(0, lambda at: land[k, 0, pl.ds(at, width), :], params)
-
-        one_out(k, slot_m2, 0, 0)
-
-        @pl.when(me < n - 1)
-        def _():
-            halo_copy(k, 0).wait_send()
-
+            send_halo(k + 1, 0)
+
+        one_out(k, u_m2, 0, 0, False)
+        halo_sent(k, 2)
         stats = finish(k, 0, stats)
-
-        @pl.when(lax.rem(k, 2) == 0)
-        def _():
-            send_halo(k + 1, 0)
-
-        @pl.when(k == 3)
-        def _():
-            out_copy(0).start()
-
         put_stats(lax.min(index + 1, 4), *stats)
 
         @pl.when(k == 1)
@@ -295,8 +306,7 @@
         return 0
 
     lax.fori_loop(0, 4, stage, 0)
-    for f in range(2):
-        out_copy(f).wait()
+    out[...] = src[...]
 
 
 def solution(mesh):
@@ -310,8 +320,8 @@
         out = pl.pallas_call(
             functools.partial(block_kernel, n, height, width, chans),
             out_shape=jax.ShapeDtypeStruct((frames, pos, chans), bf16),
-            in_specs=[pl.BlockSpec(memory_space=pl.ANY)] * 7,
-            out_specs=pl.BlockSpec(memory_space=pl.ANY),
+            in_specs=[pl.BlockSpec(memory_space=pltpu.HBM)] * 7,
+            out_specs=pl.BlockSpec(memory_space=pltpu.VMEM),
             scratch_shapes=[
                 pltpu.VMEM((4, 27, chans, chans), bf16),
                 pltpu.VMEM((4, chans, chans), bf16),
@@ -319,26 +329,36 @@
                 pltpu.VMEM((5, chans), f32),
                 pltpu.VMEM((5, chans), f32),
                 pltpu.VMEM((4, chans), f32),
-                pltpu.VMEM((4, pos + 2 * width, chans), bf16),
+                pltpu.VMEM((pos + 2 * width, chans), bf16),
+                pltpu.VMEM((pos + 2 * width, chans), bf16),
+                pltpu.VMEM((pos + 2 * width, chans), bf16),
+                pltpu.VMEM((pos + 2 * width, chans), bf16),
                 pltpu.VMEM((2, pos, chans), bf16),
                 pltpu.VMEM((2, pos, chans), bf16),
                 pltpu.VMEM((4, 2, pos, chans), bf16),
-                pltpu.VMEM((3, pos, 2 * chans), f32),
+                pltpu.VMEM((pos, 2 * chans), f32),
                 pltpu.VMEM((pos, 3 * chans), bf16),
                 pltpu.VMEM((5, 8, 128), f32),
                 pltpu.VMEM((5, n, 8, 128), f32),
                 pltpu.SemaphoreType.DMA((4,)),
                 pltpu.SemaphoreType.DMA((5,)),
                 pltpu.SemaphoreType.DMA((2,)),
-                pltpu.SemaphoreType.DMA((2,)),
-                pltpu.SemaphoreType.DMA((4, 2)),
-                pltpu.SemaphoreType.DMA((4, 2)),
+                pltpu.SemaphoreType.DMA((4, 3)),
+                pltpu.SemaphoreType.DMA((4, 3)),
                 pltpu.SemaphoreType.DMA((5, n)),
                 pltpu.SemaphoreType.DMA((5, n)),
             ],
-            compiler_params=pltpu.CompilerParams(collective_id=0, has_side_effects=True, vmem_limit_bytes=67043328),
+            compiler_params=pltpu.CompilerParams(collective_id=0, has_side_effects=True, vmem_limit_bytes=55000000),
             name="mid_block",
         )(latent.reshape(frames, pos, chans), conv_w.reshape(4, 27, chans, chans), conv_b, norm_g, norm_b, attn_w, attn_b)
+        out = pl.pallas_call(
+            copy_kernel,
+            out_shape=jax.ShapeDtypeStruct((frames, pos, chans), bf16),
+            in_specs=[pl.BlockSpec(memory_space=pltpu.VMEM)],
+            out_specs=pl.BlockSpec(memory_space=pl.ANY),
+            scratch_shapes=[pltpu.SemaphoreType.DMA],
+            name="write_out",
+        )(out)
         return out.reshape(latent.shape)
 
     return jax.shard_map(device_body, mesh=mesh, in_specs=(video_spec, P(), P(), P(), P(), P(), P()), out_specs=video_spec, check_vma=False)

time: 152 us -> 108 us (0.71)
  the two profiles are of different devices: /device:TPU:0 before, /device:TPU:5 now
where the time goes in v2:
time: 108 us; the launch traced here: 107 us
  Pallas kernels  103 us (95%)
  local copies, waits for them, and re-layouts  3.81 us (4%)
    pallas_call x1, Pallas kernels, device_body(): pl.pallas_call(functools.partial(block_kernel, n, height, width, chans),...  101 us
    unnamed x10, local copies, waits for them, and re-layouts  3.81 us
    pallas_call x1, Pallas kernels, device_body(): pl.pallas_call(copy_kernel, out_shape=jax.ShapeDtypeStruct((frames, pos,...  2.29 us

profile of v2, /device:TPU:5, one launch (start us, length us, event | category | flops | bytes accessed | tf_op | source)
XLA Modules:
  0.0 107.3 jit_solution(4688814314177966973)
XLA Ops:
  0.0 0.0 copy-start.1
  0.0 0.7 copy-done.1
  0.7 0.0 copy-start.2
  0.7 0.7 copy-done.2
  1.4 0.0 copy-start.3
  1.4 0.7 copy-done.3
  2.1 0.0 copy-start.4
  2.1 0.7 copy-done.4
  2.8 101.2 %mid_block.1.a = bf16[2,768,384]{2,1,0:T(8,128)(2,1)S(1)} custom-call(bf16[2,768,384]{2,1,0:T(8,128)(2,1)} %bitcast.4, bf16[4,27,384,384]{3,2,1,0:T(8,128)(2,1)} %bitcast.3, f32[4,384]{1,0:T(4,128)S(1)} %copy-done.3, f32[5,384]{1,0:T(8,128)S(1)} %copy-done.1, f32[5,384]{1,0:T(8,128)S(1)} %copy-done.2, bf16[4,384,384]{2,1,0:T(8,128)(2,1)} %attn_w.1, ...), custom_call_target="tpu_custom_call" | custom-call | tf_op jit(solution)/shard_map/mid_block/pallas_call | solution.py:320
  104.0 0.0 copy-start
  104.0 1.0 copy-done
  105.0 2.3 %write_out.1 = bf16[2,768,384]{2,1,0:T(8,128)(2,1)} custom-call(bf16[2,768,384]{2,1,0:T(8,128)(2,1)} %copy-done), custom_call_target="tpu_custom_call" | custom-call | tf_op jit(solution)/shard_map/write_out/pallas_call | solution.py:354
Async XLA Ops:
  0.0 0.7 copy-start.1
  0.7 0.7 copy-start.2
  1.4 0.7 copy-start.3
  2.1 0.7 copy-start.4
  104.0 1.0 copy-start

commit v3 on v2

--- a/solution.py
+++ b/solution.py
@@ -51,10 +51,6 @@
         x_copy(f).start()
     for c in small:
         c.start()
-    for k in range(4):
-        w_copy(k).start()
-    aw_copy.start()
-
     barrier = pltpu.get_barrier_semaphore()
     for d in range(1, n):
         pl.semaphore_signal(barrier, inc=1, device_id={"time": lax.rem(me + d, n)}, device_id_type=MESH)
@@ -131,8 +127,8 @@
     def halo(k, f):
         return lambda at: jnp.where(me == 0, src[0, at : at + width, :], land[k, f, at : at + width, :])
 
-    half = pos // 2
-    parts = ((1, 0, half), (1, half, half), (0, 0, pos))
+    early = 2 * width
+    parts = ((1, 0, early), (1, early, pos - early), (0, 0, pos))
 
     def halo_copy(k, part):
         f, at, rows = parts[part]
@@ -257,6 +253,11 @@
 
     for f in range(2):
         x_copy(f).wait()
+    for c in small:
+        c.wait()
+    for k in range(4):
+        w_copy(k).start()
+    aw_copy.start()
 
     def first_row(i, carry):
         for f in range(2):
@@ -267,8 +268,6 @@
         return carry
 
     put_stats(0, *lax.fori_loop(0, height, first_row, zero_stats))
-    for c in small:
-        c.wait()
     pl.semaphore_wait(barrier, n - 1)
     send_halo(0, 0)
 
@@ -279,14 +278,16 @@
         w_copy(k).wait()
         fill(u_0, own(0), params)
         one_out(k, u_1, 2, 1, True)
+        both_outs(k, 0, 0, first=True)
+        both_outs(k, 1, 0)
         halo_here(k, 0, 1)
-        both_outs(k, 0, 0, first=True)
         fill(u_m1, halo(k, 1), params)
+        both_outs(k, 2, 0)
         both_outs(k, 0, 1)
-        both_outs(k, 1, 0, 1)
+        both_outs(k, 1, 1)
         halo_here(k, 2)
         fill(u_m2, halo(k, 0), params)
-        both_outs(k, 2, 0, 1)
+        both_outs(k, 2, 1)
         halo_sent(k, 0, 1)
         stats = finish(k, 1, zero_stats)
 
@@ -320,7 +321,7 @@
         out = pl.pallas_call(
             functools.partial(block_kernel, n, height, width, chans),
             out_shape=jax.ShapeDtypeStruct((frames, pos, chans), bf16),
-            in_specs=[pl.BlockSpec(memory_space=pltpu.HBM)] * 7,
+            in_specs=[pl.BlockSpec(memory_space=pl.ANY)] * 7,
             out_specs=pl.BlockSpec(memory_space=pltpu.VMEM),
             scratch_shapes=[
                 pltpu.VMEM((4, 27, chans, chans), bf16),
@@ -350,15 +351,7 @@
             ],
             compiler_params=pltpu.CompilerParams(collective_id=0, has_side_effects=True, vmem_limit_bytes=55000000),
             name="mid_block",
-        )(latent.reshape(frames, pos, chans), conv_w.reshape(4, 27, chans, chans), conv_b, norm_g, norm_b, attn_w, attn_b)
-        out = pl.pallas_call(
-            copy_kernel,
-            out_shape=jax.ShapeDtypeStruct((frames, pos, chans), bf16),
-            in_specs=[pl.BlockSpec(memory_space=pltpu.VMEM)],
-            out_specs=pl.BlockSpec(memory_space=pl.ANY),
-            scratch_shapes=[pltpu.SemaphoreType.DMA],
-            name="write_out",
-        )(out)
+        )(*(pltpu.with_memory_space_constraint(x, pltpu.HBM) for x in (latent.reshape(frames, pos, chans), conv_w.reshape(4, 27, chans, chans), conv_b, norm_g, norm_b, attn_w, attn_b)))
         return out.reshape(latent.shape)
 
     return jax.shard_map(device_body, mesh=mesh, in_specs=(video_spec, P(), P(), P(), P(), P(), P()), out_specs=video_spec, check_vma=False)

time: 108 us -> 94.6 us (0.88)
  the two profiles are of different devices: /device:TPU:5 before, /device:TPU:0 now
where the time goes in v3:
time: 94.6 us; the launch traced here: 94.5 us
  Pallas kernels  93.5 us (99%)
  local copies, waits for them, and re-layouts  1.02 us (1%)
    pallas_call x1, Pallas kernels, device_body(): pl.pallas_call(functools.partial(block_kernel, n, height, width, chans),...  93.5 us

profile of v3, /device:TPU:0, one launch (start us, length us, event | category | flops | bytes accessed | tf_op | source)
XLA Modules:
  0.0 94.5 jit_solution(4169555063651916553)
XLA Ops:
  0.0 93.5 %mid_block.1 = bf16[2,768,384]{2,1,0:T(8,128)(2,1)S(1)} custom-call(bf16[2,768,384]{2,1,0:T(8,128)(2,1)} %bitcast.5, bf16[4,27,384,384]{3,2,1,0:T(8,128)(2,1)} %bitcast.4, f32[4,384]{1,0:T(4,128)} %conv_b.1, f32[5,384]{1,0:T(8,128)} %norm_g.1, f32[5,384]{1,0:T(8,128)} %norm_b.1, bf16[4,384,384]{2,1,0:T(8,128)(2,1)} %attn_w.1, f32[4,384]{1,0:T(4,128)} %attn_b.1), custom_call_target="tpu_custom_call" | custom-call | tf_op jit(solution)/shard_map/mid_block/pallas_call | solution.py:321
  93.5 1.0 %copy.9 = bf16[2,6,128,384]{3,2,1,0:T(8,128)(2,1)} copy(bf16[2,6,128,384]{3,2,1,0:T(8,128)(2,1)S(1)} %bitcast.3) | data formatting | bytes 2359296

commit v4 on v3

--- a/solution.py
+++ b/solution.py
@@ -9,6 +9,7 @@
 
 GROUPS = 32
 NORM_EPS = 1e-6
+LOG2E = 1.4426950408889634
 MESH = pl.DeviceIdType.MESH
 
 
@@ -127,7 +128,7 @@
     def halo(k, f):
         return lambda at: jnp.where(me == 0, src[0, at : at + width, :], land[k, f, at : at + width, :])
 
-    early = 2 * width
+    early = 3 * width
     parts = ((1, 0, early), (1, early, pos - early), (0, 0, pos))
 
     def halo_copy(k, part):
@@ -182,9 +183,10 @@
 
     outs = [slice(o * chans, (o + 1) * chans) for o in range(2)]
 
-    def one_out(k, u, a, o, first):
+    def one_out(k, frames, o, first):
         for span in spans:
-            part = dot(lhs(span, u), jnp.concatenate([rhs(span, k, a, e) for e in range(3)], axis=1))
+            w = [jnp.concatenate([rhs(span, k, a, e) for e in range(3)], axis=1) for _, a in frames]
+            part = dot(lhs(span, *(u for u, _ in frames)), jnp.concatenate(w, axis=0))
             for e in range(3):
                 add_shifted(span, part[:, e * chans : (e + 1) * chans], e, outs[o], first and e == 0)
 
@@ -211,45 +213,36 @@
     def attention():
         params = norm_params(2)
         aw_copy.wait()
-        part_rows = pos // 3
-
-        def frame(t, carry):
-            f = 1 - t
-
-            def project(i, _):
-                at = pl.ds(pl.multiple_of(i * part_rows, part_rows), part_rows)
-                a = normed(xres[f, at, :], params).astype(jnp.bfloat16)
-                w = jnp.concatenate([awbuf[0], awbuf[1], awbuf[2]], axis=1)
-                b = jnp.concatenate([abuf[j : j + 1] for j in range(3)], axis=1)
-                qkv[at, :] = (dot(a, w) + b).astype(jnp.bfloat16)
-                return 0
-
-            lax.fori_loop(0, 3, project, 0)
-
-            def attend(i, carry):
-                at = pl.ds(pl.multiple_of(i * part_rows, part_rows), part_rows)
+        rows = pos // 3
+        w = jnp.concatenate([awbuf[j] for j in range(3)], axis=1)
+        b = jnp.concatenate([abuf[j : j + 1] for j in range(3)], axis=1)
+        for f in (1, 0):
+            u = (u_0, u_1)[f]
+            for i in range(height):
+                at = slice(i * width, (i + 1) * width)
+                u[at, :] = normed(xres[f, at, :], params).astype(jnp.bfloat16)
+            qkv[f] = (dot(u[0:pos, :], w) + b).astype(jnp.bfloat16)
+        stats = zero_stats
+        for f in (1, 0):
+            for i in range(3):
+                at = slice(i * rows, (i + 1) * rows)
                 scores = lax.dot_general(
-                    qkv[at, 0:chans], qkv[:, chans : 2 * chans], (((1,), (1,)), ((), ())), preferred_element_type=jnp.float32
-                ) * chans ** -0.5
+                    qkv[f, at, 0:chans], qkv[f, :, chans : 2 * chans], (((1,), (1,)), ((), ())), preferred_element_type=jnp.float32
+                )
                 top = jnp.max(scores, axis=1, keepdims=True)
-                e = jnp.exp(scores - top)
-                p = (e / jnp.sum(e, axis=1, keepdims=True)).astype(jnp.bfloat16)
-                o = dot(p, qkv[:, 2 * chans : 3 * chans]).astype(jnp.bfloat16)
+                e = jnp.exp2((scores - top) * (chans ** -0.5 * LOG2E))
+                p = (e * (1.0 / jnp.sum(e, axis=1, keepdims=True))).astype(jnp.bfloat16)
+                o = dot(p, qkv[f, :, 2 * chans : 3 * chans]).astype(jnp.bfloat16)
                 h = (dot(o, awbuf[3]) + abuf[3:4]).astype(jnp.bfloat16)
                 new = (xres[f, at, :].astype(jnp.float32) + h.astype(jnp.float32)).astype(jnp.bfloat16)
                 src[f, at, :] = new
                 xres[f, at, :] = new
-                return add_stats(carry, new.astype(jnp.float32))
-
-            carry = lax.fori_loop(0, 3, attend, carry)
-
-            @pl.when(t == 0)
-            def _():
+                stats = add_stats(stats, new.astype(jnp.float32))
+            if f == 1:
                 send_halo(2, 0)
-
-            return carry
-
-        put_stats(3, *lax.fori_loop(0, 2, frame, zero_stats))
+        put_stats(3, *stats)
+        for u in (u_0, u_1):
+            u[0:width, :] = jnp.zeros((width, chans), jnp.bfloat16)
 
     for f in range(2):
         x_copy(f).wait()
@@ -274,28 +267,26 @@
     def stage(k, _):
         index = k + lax.div(k, 2)
         params = norm_params(index, lambda: send_halo(k, 1, 2))
+        w_copy(k).wait()
         fill(u_1, own(1), params)
-        w_copy(k).wait()
         fill(u_0, own(0), params)
-        one_out(k, u_1, 2, 1, True)
+        one_out(k, ((u_1, 2),), 1, True)
         both_outs(k, 0, 0, first=True)
         both_outs(k, 1, 0)
         halo_here(k, 0, 1)
         fill(u_m1, halo(k, 1), params)
         both_outs(k, 2, 0)
-        both_outs(k, 0, 1)
-        both_outs(k, 1, 1)
+        one_out(k, ((u_m1, 0),), 1, False)
+        halo_sent(k, 0, 1)
+        stats = finish(k, 1, zero_stats)
+
+        @pl.when(lax.rem(k, 2) == 0)
+        def _():
+            send_halo(k + 1, 0)
+
         halo_here(k, 2)
         fill(u_m2, halo(k, 0), params)
-        both_outs(k, 2, 1)
-        halo_sent(k, 0, 1)
-        stats = finish(k, 1, zero_stats)
-
-        @pl.when(lax.rem(k, 2) == 0)
-        def _():
-            send_halo(k + 1, 0)
-
-        one_out(k, u_m2, 0, 0, False)
+        one_out(k, ((u_m1, 1), (u_m2, 0)), 0, False)
         halo_sent(k, 2)
         stats = finish(k, 0, stats)
         put_stats(lax.min(index + 1, 4), *stats)
@@ -338,7 +329,7 @@
                 pltpu.VMEM((2, pos, chans), bf16),
                 pltpu.VMEM((4, 2, pos, chans), bf16),
                 pltpu.VMEM((pos, 2 * chans), f32),
-                pltpu.VMEM((pos, 3 * chans), bf16),
+                pltpu.VMEM((2, pos, 3 * chans), bf16),
                 pltpu.VMEM((5, 8, 128), f32),
                 pltpu.VMEM((5, n, 8, 128), f32),
                 pltpu.SemaphoreType.DMA((4,)),

time: 94.6 us -> 90.4 us (0.956)
  Pallas kernels: 93.5 us -> 89.2 us
    pallas_call x1, Pallas kernels: 93.5 us -> 89.2 us  [device_body(): pl.pallas_call(functools.partial(block_kernel, n, height, width, chans),...]
where the time goes in v4:
time: 90.4 us; the launch traced here: 90.3 us
  Pallas kernels  89.2 us (99%)
  local copies, waits for them, and re-layouts  1.02 us (1%)
    pallas_call x1, Pallas kernels, device_body(): pl.pallas_call(functools.partial(block_kernel, n, height, width, chans),...  89.2 us

profile of v4, /device:TPU:0, one launch (start us, length us, event | category | flops | bytes accessed | tf_op | source)
XLA Modules:
  0.0 90.3 jit_solution(5547140753254050240)
XLA Ops:
  0.0 89.2 %mid_block.1 = bf16[2,768,384]{2,1,0:T(8,128)(2,1)S(1)} custom-call(bf16[2,768,384]{2,1,0:T(8,128)(2,1)} %bitcast.5, bf16[4,27,384,384]{3,2,1,0:T(8,128)(2,1)} %bitcast.4, f32[4,384]{1,0:T(4,128)} %conv_b.1, f32[5,384]{1,0:T(8,128)} %norm_g.1, f32[5,384]{1,0:T(8,128)} %norm_b.1, bf16[4,384,384]{2,1,0:T(8,128)(2,1)} %attn_w.1, f32[4,384]{1,0:T(4,128)} %attn_b.1), custom_call_target="tpu_custom_call" | custom-call | tf_op jit(solution)/shard_map/mid_block/pallas_call | solution.py:312
  89.2 1.0 %copy.9 = bf16[2,6,128,384]{3,2,1,0:T(8,128)(2,1)} copy(bf16[2,6,128,384]{3,2,1,0:T(8,128)(2,1)S(1)} %bitcast.3) | data formatting | bytes 2359296

commit v5 on v4

--- a/solution.py
+++ b/solution.py
@@ -184,7 +184,7 @@
     outs = [slice(o * chans, (o + 1) * chans) for o in range(2)]
 
     def one_out(k, frames, o, first):
-        for span in spans:
+        for span in (spans[1], spans[0], spans[2]) if first else spans:
             w = [jnp.concatenate([rhs(span, k, a, e) for e in range(3)], axis=1) for _, a in frames]
             part = dot(lhs(span, *(u for u, _ in frames)), jnp.concatenate(w, axis=0))
             for e in range(3):
@@ -248,9 +248,7 @@
         x_copy(f).wait()
     for c in small:
         c.wait()
-    for k in range(4):
-        w_copy(k).start()
-    aw_copy.start()
+    w_copy(0).start()
 
     def first_row(i, carry):
         for f in range(2):
@@ -268,6 +266,15 @@
         index = k + lax.div(k, 2)
         params = norm_params(index, lambda: send_halo(k, 1, 2))
         w_copy(k).wait()
+
+        @pl.when(k < 3)
+        def _():
+            w_copy(lax.min(k + 1, 3)).start()
+
+        @pl.when(k == 0)
+        def _():
+            aw_copy.start()
+
         fill(u_1, own(1), params)
         fill(u_0, own(0), params)
         one_out(k, ((u_1, 2),), 1, True)

time: 90.4 us -> 90 us (level)
  no operation moved by 1% of the time
where the time goes in v5:
time: 90 us; the launch traced here: 89.9 us
  Pallas kernels  88.9 us (99%)
  local copies, waits for them, and re-layouts  1.02 us (1%)
    pallas_call x1, Pallas kernels, device_body(): pl.pallas_call(functools.partial(block_kernel, n, height, width, chans),...  88.9 us

profile of v5, /device:TPU:0, one launch (start us, length us, event | category | flops | bytes accessed | tf_op | source)
XLA Modules:
  0.0 89.9 jit_solution(13408259791950438187)
XLA Ops:
  0.0 88.9 %mid_block.1 = bf16[2,768,384]{2,1,0:T(8,128)(2,1)S(1)} custom-call(bf16[2,768,384]{2,1,0:T(8,128)(2,1)} %bitcast.5, bf16[4,27,384,384]{3,2,1,0:T(8,128)(2,1)} %bitcast.4, f32[4,384]{1,0:T(4,128)} %conv_b.1, f32[5,384]{1,0:T(8,128)} %norm_g.1, f32[5,384]{1,0:T(8,128)} %norm_b.1, bf16[4,384,384]{2,1,0:T(8,128)(2,1)} %attn_w.1, f32[4,384]{1,0:T(4,128)} %attn_b.1), custom_call_target="tpu_custom_call" | custom-call | tf_op jit(solution)/shard_map/mid_block/pallas_call | solution.py:319
  88.9 1.0 %copy.9 = bf16[2,6,128,384]{3,2,1,0:T(8,128)(2,1)} copy(bf16[2,6,128,384]{3,2,1,0:T(8,128)(2,1)S(1)} %bitcast.3) | data formatting | bytes 2359296
